TPU v7x, 128 devices: a whole 4x4x4 slice. The times are simulated.
128 devices in a mesh: node: 8 (over x, core), local: 16 (over y, z).
Axes of the slice: x: 4, y: 4, z: 4, core: 2. Of those that a mesh axis runs over, the one named last changes fastest.
Arguments:
- tokens: bfloat16 [8192, 7168], P(('node', 'local')), may hold values from -6 to 6
- routes: int32 [8192, 2], P(('node', 'local')), may hold values from 0 to 31, as said below
- scores: float32 [8192, 2], P(('node', 'local')), may hold values from 0.1 to 1
- gate_proj: bfloat16 [128, 7168, 512], P(('node', 'local')), may hold values from -0.0625 to 0.0625
- up_proj: bfloat16 [128, 7168, 512], P(('node', 'local')), may hold values from -0.0625 to 0.0625
- down_proj: bfloat16 [128, 512, 7168], P(('node', 'local')), may hold values from -0.125 to 0.125
Outputs:
- combined: bfloat16 [8192, 7168], P(('node', 'local'))
Inputs may be any that keep to these rules, and one draw needn't show every extreme that they name: `routes`: each row names 2 different experts. The rows of one device name each expert at most 5 times, and in every draw one expert is named by exactly 5 rows of every device.
All inputs are finite; a program needn't handle non-finite values.
Results may differ from a plain program's by a relative error of at most 0.0085.
Values may be sent and summed in bfloat16 or wider, within the bound.
A program may use at most 192 MiB of HBM per device.

v0:
```python
import jax
import jax.numpy as jnp
from jax import lax
from jax.sharding import PartitionSpec as P

SHARDS = 4


SCALE = 2.827


def expert_block(block_rows, w_gate, w_up, w_down):
    block_shape = block_rows.shape
    flat_rows = block_rows.reshape(-1, block_shape[-1])
    gate_act = jnp.dot(flat_rows, w_gate, preferred_element_type=jnp.float32)
    up_act = jnp.dot(flat_rows, w_up, preferred_element_type=jnp.float32)
    hidden = (jax.nn.silu(gate_act) * up_act).astype(jnp.bfloat16)
    partial_value = jnp.dot(hidden, w_down, preferred_element_type=jnp.float32).astype(jnp.bfloat16)
    return partial_value.reshape(block_shape[:-1] + (w_down.shape[1],))


def per_device(tokens, routes, scores, gate_proj, up_proj, down_proj):
    node_count = lax.axis_size("node")
    local_count = lax.axis_size("local")
    token_count, model_width = tokens.shape
    top_count = routes.shape[1]
    node_experts = local_count // SHARDS
    experts = node_count * node_experts
    per_expert = max(
        2, token_count * top_count // experts + token_count * top_count // (4 * experts)
    )
    w_gate = gate_proj[0]
    w_up = up_proj[0]
    w_down = down_proj[0]
    weights = (SCALE * scores / jnp.sum(scores, axis=1, keepdims=True)).astype(jnp.bfloat16)
    labels = jnp.arange(experts, dtype=jnp.int32)
    matches = routes[:, :, None] == labels[None, None, :]
    dense_weight = jnp.sum(jnp.where(matches, weights.astype(jnp.float32)[:, :, None], 0.0), axis=1)
    node_cap = min(token_count, node_experts * per_expert)
    grouped = dense_weight.reshape(token_count, node_count, node_experts)
    reached = jnp.any(grouped > 0, axis=2)
    node_slot = jnp.cumsum(reached.astype(jnp.int32), axis=0) - 1
    slot_index = jnp.arange(node_cap, dtype=jnp.int32)
    node_pick = reached[None] & (node_slot[None] == slot_index[:, None, None])
    send_rows = jnp.einsum(
        "ctn,td->ncd", node_pick.astype(jnp.bfloat16), tokens, preferred_element_type=jnp.float32
    ).astype(jnp.bfloat16)
    send_weight = jnp.einsum(
        "ctn,tnj->ncj", node_pick.astype(jnp.float32), grouped, precision=lax.Precision.HIGHEST
    ).astype(jnp.bfloat16)
    arrived, arrived_weight = (
        lax.all_to_all(send_rows, "node", split_axis=0, concat_axis=0, tiled=True),
        lax.all_to_all(send_weight, "node", split_axis=0, concat_axis=0, tiled=True),
    )
    row_count = node_count * node_cap
    arrived = arrived.reshape(row_count, model_width)
    row_weight = arrived_weight.reshape(row_count, node_experts).astype(jnp.float32)
    capacity = node_count * per_expert
    routed = row_weight > 0
    position = jnp.cumsum(routed.astype(jnp.int32), axis=0) - 1
    slot_ids = jnp.arange(capacity, dtype=jnp.int32)
    slot_pick = (routed[None] & (position[None] == slot_ids[:, None, None])).astype(jnp.bfloat16)
    bucket = jnp.einsum(
        "crj,rd->jcd", slot_pick, arrived, preferred_element_type=jnp.float32
    ).astype(jnp.bfloat16)
    outgoing = jnp.broadcast_to(
        bucket[:, None], (node_experts, SHARDS, capacity, model_width)
    ).reshape(local_count, capacity, model_width)
    results = expert_block(
        lax.all_to_all(outgoing, "local", split_axis=0, concat_axis=0, tiled=True),
        w_gate,
        w_up,
        w_down,
    )
    returned = lax.all_to_all(results, "local", split_axis=0, concat_axis=0, tiled=True)
    summed = jnp.sum(
        returned.reshape(node_experts, SHARDS, capacity, model_width).astype(jnp.float32), axis=1
    )
    local_ids = jnp.arange(node_experts, dtype=jnp.int32)
    gathered = summed[local_ids[None, :], jnp.clip(position, 0, capacity - 1)]
    node_total = jnp.sum(gathered * row_weight[:, :, None], axis=1).reshape(
        node_count, node_cap, model_width
    )
    returned_home = lax.all_to_all(
        node_total.astype(jnp.bfloat16), "node", split_axis=0, concat_axis=0, tiled=True
    ).astype(node_total.dtype)
    node_ids = jnp.arange(node_count, dtype=jnp.int32)
    gathered_home = returned_home[node_ids[None, :], jnp.clip(node_slot, 0, node_cap - 1)]
    combined = jnp.sum(jnp.where(reached[:, :, None], gathered_home, 0.0), axis=1)
    return combined.astype(jnp.bfloat16)


def solution(mesh):
    return jax.shard_map(
        per_device,
        mesh=mesh,
        in_specs=(
            P(("node", "local"), None),
            P(("node", "local"), None),
            P(("node", "local"), None),
            P(("node", "local"), None, None),
            P(("node", "local"), None, None),
            P(("node", "local"), None, None),
        ),
        out_specs=P(("node", "local"), None),
        check_vma=False,
    )
```

profile of v0, /device:TPU:1, one launch (start us, length us, event | category | flops | bytes accessed | tf_op | source)
XLA Modules:
  0.0 520.3 jit_solution(17380416106367744728)
XLA Ops:
  3.3 5.8 %all-to-all-start.1 = ((bf16[8,20,4]{1,2,0:T(4,128)(2,1)}), bf16[8,20,4]{1,2,0:T(4,128)(2,1)S(1)}, u32[]{:S(2)}, u32[]{:S(2)}) async-start(bf16[8,20,4]{1,2,0:T(4,128)(2,1)} %convolution_convert_fusion.3), calls=%async_computation.1 | async-start | bytes 16384 | tf_op jit(solution)/shard_map/all_to_all | solution.py:53
  9.8 2.9 copy.70
  13.7 5.0 all-to-all-start
  18.8 1.2 reduce-window.6
  20.6 31.4 %all-to-all-done = bf16[8,20,7168]{2,1,0:T(8,128)(2,1)} async-done(((bf16[8,20,7168]{2,1,0:T(8,128)(2,1)}), bf16[8,20,7168]{2,1,0:T(8,128)(2,1)}, u32[]{:S(2)}, u32[]{:S(2)}) %all-to-all-start) | async-done | bytes 2293792 | tf_op jit(solution)/shard_map/all_to_all | solution.py:52
  52.0 2.7 reshape.113
  54.8 2.1 fusion.2
  56.9 2.9 broadcast_in_dim.31
  59.8 110.2 %all_to_all.25 = bf16[16,40,7168]{2,1,0:T(8,128)(2,1)S(1)} all-to-all(bf16[16,40,7168]{2,1,0:T(8,128)(2,1)S(1)} %bitcast.54), channel_id=1, replica_groups=mesh['node'=8,'local'=16] {'local'}, dimensions={0} | all-to-all | bytes 18350080 | tf_op jit(solution)/shard_map/all_to_all | solution.py:70
  169.9 7.4 %fusion.6 = f32[640,512]{1,0:T(8,128)S(1)} fusion(bf16[640,7168]{1,0:T(8,128)(2,1)S(1)} %bitcast.56, bf16[1,7168,512]{2,1,0:T(8,128)(2,1)} %param.9), kind=kOutput, calls=%fused_computation.14 | convolution fusion | flops 4697620480 | bytes 17825792 | tf_op jit(solution)/shard_map/dot_general | solution.py:15
  177.4 5.0 fusion.11
  182.5 7.3 %convolution_convert_fusion = bf16[640,7168]{1,0:T(8,128)(2,1)} fusion(bf16[640,512]{1,0:T(8,128)(2,1)S(1)} %fusion.11, bf16[1,512,7168]{2,1,0:T(8,128)(2,1)S(1)} %bitcast.66), kind=kOutput, calls=%fused_computation.6 | convolution fusion | flops 4702208000 | bytes 17170432 | tf_op jit(solution)/shard_map/dot_general | solution.py:18
  189.8 5.0 all-to-all-start.3
  195.0 143.2 %all-to-all-done.3 = bf16[16,40,7168]{2,1,0:T(8,128)(2,1)} async-done(((bf16[16,40,7168]{2,1,0:T(8,128)(2,1)}), bf16[16,40,7168]{2,1,0:T(8,128)(2,1)}, u32[]{:S(2)}, u32[]{:S(2)}) %all-to-all-start.3) | async-done | bytes 9175072 | tf_op jit(solution)/shard_map/all_to_all | solution.py:75
  338.3 8.1 %convert_reduce_fusion = f32[4,40,7168]{2,1,0:T(8,128)} fusion(bf16[16,40,7168]{2,1,0:T(8,128)(2,1)} %all-to-all-done.3), kind=kLoop, calls=%fused_computation.2 | loop fusion | flops 8028160 | bytes 13762560 | tf_op jit(solution)/shard_map/reduce_sum | solution.py:76
  346.3 47.3 %gather_fusion = f32[640,7168]{1,0:T(8,128)} fusion(f32[4,40,7168]{2,1,0:T(8,128)} %convert_reduce_fusion, s32[640]{0:T(1024)S(1)} %reshape.95), kind=kCustom, calls=%fused_computation | custom fusion | bytes 36705280 | tf_op jit(solution)/shard_map/gather | solution.py:80
  393.6 20.0 %reshape.98 = f32[160,4,7168]{2,1,0:T(4,128)} reshape(f32[640,7168]{1,0:T(8,128)} %gather_fusion) | data formatting | bytes 36700160 | tf_op jit(solution)/shard_map/gather | solution.py:80
  413.6 15.5 %multiply_reduce_fusion = bf16[160,7168]{1,0:T(8,128)(2,1)S(1)} fusion(f32[160,4,7168]{2,1,0:T(4,128)} %reshape.98, f32[160,4]{1,0:T(8,128)S(1)} %copy.76), kind=kLoop, calls=%fused_computation.3 | loop fusion | flops 8028160 | bytes 20646400 | tf_op jit(solution)/shard_map/reduce_sum | solution.py:81
  429.2 2.2 convert_element_type.81
  431.4 10.1 %all-to-all-start.4 = ((bf16[8,20,7168]{2,1,0:T(8,128)(2,1)}), bf16[8,20,7168]{2,1,0:T(8,128)(2,1)}, u32[]{:S(2)}, u32[]{:S(2)}) async-start(bf16[8,20,7168]{2,1,0:T(8,128)(2,1)} %convert_element_type.81), calls=%async_computation.4 | async-start | bytes 5505024 | tf_op jit(solution)/shard_map/all_to_all | solution.py:84
  441.7 33.1 %all-to-all-done.4 = bf16[8,20,7168]{2,1,0:T(8,128)(2,1)} async-done(((bf16[8,20,7168]{2,1,0:T(8,128)(2,1)}), bf16[8,20,7168]{2,1,0:T(8,128)(2,1)}, u32[]{:S(2)}, u32[]{:S(2)}) %all-to-all-start.4) | async-done | bytes 2293792 | tf_op jit(solution)/shard_map/all_to_all | solution.py:84
  474.9 5.2 copy_convert_fusion
  480.0 28.6 %gather_fusion.1 = f32[512,7168]{1,0:T(8,128)} fusion(f32[8,20,7168]{2,0,1:T(8,128)} %copy_convert_fusion, s32[512]{0:T(512)S(1)} %reshape.101), kind=kCustom, calls=%fused_computation.1 | custom fusion | bytes 29364224 | tf_op jit(solution)/shard_map/gather | solution.py:88
  508.7 11.6 %fusion = bf16[64,7168]{1,0:T(8,128)(2,1)} fusion(f32[512,7168]{1,0:T(8,128)} %gather_fusion.1, pred[64,8]{1,0:T(8,128)(4,1)S(1)} %copy.66), kind=kLoop, calls=%fused_computation.5 | loop fusion | flops 6881280 | bytes 15598080 | tf_op jit(solution)/shard_map/reduce_sum | solution.py:89
  (48 shorter events, 6.2 us)
Async XLA Ops:
  0.0 9.1 %copy-start = (bf16[64,7168]{1,0:T(8,128)(2,1)S(1)}, bf16[64,7168]{1,0:T(8,128)(2,1)}, u32[]{:S(2)}) copy-start(bf16[64,7168]{1,0:T(8,128)(2,1)} %param.6) | copy-start | bytes 2752516
  3.3 10.4 %all-to-all-start.1 = ((bf16[8,20,4]{1,2,0:T(4,128)(2,1)}), bf16[8,20,4]{1,2,0:T(4,128)(2,1)S(1)}, u32[]{:S(2)}, u32[]{:S(2)}) async-start(bf16[8,20,4]{1,2,0:T(4,128)(2,1)} %convolution_convert_fusion.3), calls=%async_computation.1 | async-start | bytes 16384 | tf_op jit(solution)/shard_map/all_to_all | solution.py:53
  13.7 38.3 %all-to-all-start = ((bf16[8,20,7168]{2,1,0:T(8,128)(2,1)}), bf16[8,20,7168]{2,1,0:T(8,128)(2,1)}, u32[]{:S(2)}, u32[]{:S(2)}) async-start(bf16[8,20,7168]{2,1,0:T(8,128)(2,1)} %copy.70), calls=%async_computation | async-start | bytes 5505024 | tf_op jit(solution)/shard_map/all_to_all | solution.py:52
  59.8 117.6 %slice-start = ((s8[7340032]{0:T(1024)(128)(4,1)}), s8[4194304]{0:T(1024)(128)(4,1)S(1)}, s32[]{:S(2)}) async-start(s8[7340032]{0:T(1024)(128)(4,1)} %bitcast.63), calls=%async_computation.5 | async-start | bytes 8388608
  169.9 7.5 %slice-start.1 = ((s8[7340032]{0:T(1024)(128)(4,1)}), s8[3145728]{0:T(1024)(128)(4,1)S(1)}, s32[]{:S(2)}) async-start(s8[7340032]{0:T(1024)(128)(4,1)} %bitcast.63), calls=%async_computation.6 | async-start | bytes 6291456
  169.9 12.5 %slice-start.2 = ((s8[7340032]{0:T(1024)(128)(4,1)}), s8[4194304]{0:T(1024)(128)(4,1)S(1)}, s32[]{:S(2)}) async-start(s8[7340032]{0:T(1024)(128)(4,1)} %bitcast.65), calls=%async_computation.7 | async-start | bytes 8388608
  177.4 5.1 slice-start.3
  189.8 148.5 %all-to-all-start.3 = ((bf16[16,40,7168]{2,1,0:T(8,128)(2,1)}), bf16[16,40,7168]{2,1,0:T(8,128)(2,1)}, u32[]{:S(2)}, u32[]{:S(2)}) async-start(bf16[16,40,7168]{2,1,0:T(8,128)(2,1)} %bitcast.55), calls=%async_computation.3 | async-start | bytes 18350080 | tf_op jit(solution)/shard_map/all_to_all | solution.py:75
  431.4 43.5 %all-to-all-start.4 = ((bf16[8,20,7168]{2,1,0:T(8,128)(2,1)}), bf16[8,20,7168]{2,1,0:T(8,128)(2,1)}, u32[]{:S(2)}, u32[]{:S(2)}) async-start(bf16[8,20,7168]{2,1,0:T(8,128)(2,1)} %convert_element_type.81), calls=%async_computation.4 | async-start | bytes 5505024 | tf_op jit(solution)/shard_map/all_to_all | solution.py:84
  480.0 40.3 %copy-start.1 = (bf16[64,7168]{1,0:T(8,128)(2,1)S(1)}, bf16[64,7168]{1,0:T(8,128)(2,1)}, u32[]{:S(2)}) copy-start(bf16[64,7168]{1,0:T(8,128)(2,1)} %param.6) | copy-start | bytes 2752516
where the time goes:
time: 524 us; the launch traced here: 520 us
  waiting for transfers between devices  209 us (40%)
  blocking collectives  110 us (21%)
  local copies, waits for them, and re-layouts  108 us (21%)
  other arithmetic  44.2 us (8%)
  starting transfers between devices  25.9 us (5%)
  matrix products  23.4 us (4%)
    all_to_all x1, waiting for transfers between devices, per_device(): lax.all_to_all(results, 'local', split_axis=0, concat_axis=0, tiled=True)  143 us
    all_to_all x1, blocking collectives, per_device(): lax.all_to_all(outgoing, 'local', split_axis=0, concat_axis=0, tiled=True)  110 us
    gather x2, local copies, waits for them, and re-layouts, per_device(): gathered = summed[local_ids[None, :], jnp.clip(position, 0, capacity - 1)]  67.3 us
    all_to_all x1, waiting for transfers between devices, per_device(): lax.all_to_all(node_total.astype(jnp.bfloat16), 'node', split_axis=0, con...  33.1 us
    all_to_all x1, waiting for transfers between devices, per_device(): lax.all_to_all(send_rows, 'node', split_axis=0, concat_axis=0, tiled=True)  31.4 us
    gather x1, local copies, waits for them, and re-layouts, per_device(): returned_home[node_ids[None, :], jnp.clip(node_slot, 0, node_cap - 1)]  28.6 us
    reduce_sum x1, other arithmetic, per_device(): jnp.sum(gathered * row_weight[:, :, None], axis=1)  15.5 us
    reduce_sum x1, other arithmetic, per_device(): jnp.sum(jnp.where(reached[:, :, None], gathered_home, 0.0), axis=1)  11.6 us
  transfers between devices with their start and end apart: 4, of which 4 were waited for; matrix products, arithmetic and copies ran while one was open for 1% of the time, Pallas kernels for 0%

commit v1 on v0

v1 whole, which is shorter than its diff:
```python
import functools

import jax
import jax.numpy as jnp
from jax import lax
from jax.experimental import pallas as pl
from jax.experimental.pallas import tpu as pltpu
from jax.sharding import PartitionSpec as P

MESH = pl.DeviceIdType.MESH
SHARDS = 4
SCALE = 2.827
MOST = 5
LANES = 128


def kernel(
    plane, rows_of, wide,
    pick_ref, home_ref, weight_ref, tok_ref, gate_hbm, up_hbm, down_hbm,
    out_ref,
    w_gate, w_up, w_down, sent, got, x_all, part, half_in, full_in, back, home, wide32, acc, hid,
    w_sem, plane_s, plane_r, ag_s, ag_r, fw_s, fw_r, rh_s, rh_r, rf_s, rf_r, back_s, back_r,
):
    node, local = lax.axis_index("node"), lax.axis_index("local")
    ys = lax.axis_size("local") // SHARDS
    y, z = local // SHARDS, local % SHARDS
    me = node * ys + y
    nxt, prv, far = (z + 1) % SHARDS, (z + 3) % SHARDS, (z + 2) % SHARDS
    up_dev = (node, y * SHARDS + nxt)
    dn_dev = (node, y * SHARDS + prv)
    subs = wide // LANES
    half = plane // 2
    depth = w_gate.shape[0]
    hidden = w_gate.shape[1]

    w_copies = [
        pltpu.make_async_copy(gate_hbm.at[0], w_gate, w_sem.at[0]),
        pltpu.make_async_copy(up_hbm.at[0], w_up, w_sem.at[1]),
        pltpu.make_async_copy(down_hbm.at[0], w_down, w_sem.at[2]),
    ]
    for copy in w_copies:
        copy.start()

    def peer(k):
        other = lax.rem(me + k, plane)
        return other, (other // ys, (other % ys) * SHARDS + z)

    barrier = pltpu.get_barrier_semaphore()

    def greet(k, carry):
        pl.semaphore_signal(barrier, inc=1, device_id=peer(k)[1], device_id_type=MESH)
        return carry

    lax.fori_loop(1, plane, greet, 0)
    for dev in (up_dev, dn_dev):
        pl.semaphore_signal(barrier, inc=1, device_id=dev, device_id_type=MESH)

    def fill(i, carry):
        c, e = i // plane, i % plane
        sent[c, e] = tok_ref[pick_ref[c, e]]
        return carry

    lax.fori_loop(0, rows_of * plane, fill, 0)
    pl.semaphore_wait(barrier, plane + 1)

    def remote(src, dst, s_sem, r_sem, dev):
        return pltpu.make_async_remote_copy(
            src_ref=src, dst_ref=dst, send_sem=s_sem, recv_sem=r_sem, device_id=dev, device_id_type=MESH
        )

    def spread(src, dst, s_sem, r_sem, c):
        def one(k, carry):
            other, dev = peer(k)
            remote(src.at[c, other], dst.at[c, me], s_sem.at[c], r_sem.at[c], dev).start()
            return carry

        lax.fori_loop(1, plane, one, 0)
        dst[c, me] = src[c, me]

    def spread_all(src, dst, s_sem, r_sem, c):
        some = pl.ds(0, plane - 1)
        return remote(src.at[c, some], dst.at[c, some], s_sem.at[c], r_sem.at[c], up_dev)

    def gather(c):
        return (
            remote(x_all.at[c, z], x_all.at[c, z], ag_s.at[c, 0], ag_r.at[c, 0], up_dev),
            remote(x_all.at[c, z], x_all.at[c, z], ag_s.at[c, 1], ag_r.at[c, 1], dn_dev),
        )

    def forward(c):
        low, high = pl.ds(0, half), pl.ds(half, half)
        return (
            remote(x_all.at[c, prv, low], x_all.at[c, prv, low], fw_s.at[c, 0], fw_r.at[c, 0], up_dev),
            remote(x_all.at[c, nxt, high], x_all.at[c, nxt, high], fw_s.at[c, 1], fw_r.at[c, 1], dn_dev),
        )

    def scatter_half(c):
        low, high = pl.ds(0, half), pl.ds(half, half)
        return (
            remote(part.at[c, far, low], half_in.at[c, 0], rh_s.at[c, 0], rh_r.at[c, 0], up_dev),
            remote(part.at[c, far, high], half_in.at[c, 1], rh_s.at[c, 1], rh_r.at[c, 1], dn_dev),
        )

    def scatter_full(c):
        return (
            remote(part.at[c, nxt], full_in.at[c, 0], rf_s.at[c, 0], rf_r.at[c, 0], up_dev),
            remote(part.at[c, prv], full_in.at[c, 1], rf_s.at[c, 1], rf_r.at[c, 1], dn_dev),
        )

    def stage_a(c):
        spread_all(sent, got, plane_s, plane_r, c).wait_recv()

        def widen(s, carry):
            wide32[pl.ds(pl.multiple_of(s * subs, 8), subs), :] = got[c, s].astype(jnp.float32)
            return carry

        lax.fori_loop(0, plane, widen, 0)

        def column(j, carry):
            cols = pl.ds(pl.multiple_of(j * LANES, LANES), LANES)
            for s0 in range(0, plane, 16):
                rows = [wide32[pl.ds((s0 + d) * subs + j, 8, stride=subs), :] for d in (0, 8)]
                x_all[c, z, pl.ds(s0, 16), cols] = jnp.concatenate(rows, axis=0).astype(jnp.bfloat16)
            return carry

        lax.fori_loop(0, subs, column, 0)
        for copy in gather(c):
            copy.start()

    def stage_b(c):
        for copy in gather(c):
            copy.wait_recv()
        for copy in forward(c):
            copy.start()

    def stage_c(c):
        for copy in forward(c):
            copy.wait_recv()
        rows = SHARDS * plane
        block = min(1024, depth)

        acc[...] = jnp.zeros_like(acc)

        def contract(k, carry):
            span = pl.ds(pl.multiple_of(k * block, LANES), block)
            rows_k = x_all[c, :, :, span].reshape(rows, block)
            acc[:, :hidden] += jnp.dot(rows_k, w_gate[span, :], preferred_element_type=jnp.float32)
            acc[:, hidden:] += jnp.dot(rows_k, w_up[span, :], preferred_element_type=jnp.float32)
            return carry

        lax.fori_loop(0, depth // block, contract, 0)
        gate = acc[:, :hidden]
        hid[...] = (gate / (1.0 + jnp.exp(-gate)) * acc[:, hidden:]).astype(jnp.bfloat16)

        def expand(k, carry):
            span = pl.ds(pl.multiple_of(k * block, LANES), block)
            value = jnp.dot(hid[...], w_down[:, span], preferred_element_type=jnp.float32)
            part[c, :, :, span] = value.astype(jnp.bfloat16).reshape(SHARDS, plane, block)
            return carry

        lax.fori_loop(0, depth // block, expand, 0)
        for copy in scatter_half(c):
            copy.start()

    def stage_e(c):
        for copy in scatter_half(c):
            copy.wait_recv()
        for side, owner, start in ((0, nxt, 0), (1, prv, half)):
            span = pl.ds(start, half)
            mine = part[c, owner, span].astype(jnp.float32)
            part[c, owner, span] = (mine + half_in[c, side].astype(jnp.float32)).astype(jnp.bfloat16)
        for copy in scatter_full(c):
            copy.start()

    def stage_f(c):
        for copy in scatter_full(c):
            copy.wait_recv()

        def column(j, carry):
            cols = pl.ds(pl.multiple_of(j * LANES, LANES), LANES)
            for s0 in range(0, plane, 16):
                span = pl.ds(s0, 16)
                value = part[c, z, span, cols].astype(jnp.float32)
                value = value + full_in[c, 0, span, cols].astype(jnp.float32)
                value = value + full_in[c, 1, span, cols].astype(jnp.float32)
                for d in (0, 8):
                    wide32[pl.ds((s0 + d) * subs + j, 8, stride=subs), :] = value[d:d + 8]
            return carry

        lax.fori_loop(0, subs, column, 0)

        def narrow(s, carry):
            back[c, s] = wide32[pl.ds(pl.multiple_of(s * subs, 8), subs), :].astype(jnp.bfloat16)
            return carry

        lax.fori_loop(0, plane, narrow, 0)
        spread(back, home, back_s, back_r, c)

    def launch(c, carry):
        spread(sent, got, plane_s, plane_r, c)
        return carry

    lax.fori_loop(0, rows_of, launch, 0)

    stages = (stage_a, stage_b, stage_c, stage_e, stage_f)

    def step(s, carry):
        @pl.when(s == 2)
        def _():
            for copy in w_copies:
                copy.wait()

        for lag, stage in enumerate(stages):
            c = s - lag

            @pl.when((c >= 0) & (c < rows_of))
            def _(stage=stage, c=c):
                stage(c)

        return carry

    lax.fori_loop(0, rows_of + len(stages) - 1, step, 0)

    def arrive(c, carry):
        spread_all(back, home, back_s, back_r, c).wait_recv()
        return carry

    lax.fori_loop(0, rows_of, arrive, 0)

    def combine(t, carry):
        total = jnp.zeros((subs, LANES), jnp.float32)
        for k in range(home_ref.shape[1]):
            spot = home_ref[t, k]
            total = total + weight_ref[t, k] * home[spot // plane, spot % plane].astype(jnp.float32)
        out_ref[t] = total.astype(jnp.bfloat16)
        return carry

    lax.fori_loop(0, out_ref.shape[0], combine, 0)

    def drain(c, carry):
        spread_all(sent, got, plane_s, plane_r, c).wait_send()
        spread_all(back, home, back_s, back_r, c).wait_send()
        for group in (gather, forward, scatter_half, scatter_full):
            for copy in group(c):
                copy.wait_send()
        return carry

    lax.fori_loop(0, rows_of, drain, 0)


def per_device(tokens, routes, scores, gate_proj, up_proj, down_proj):
    plane = lax.axis_size("node") * (lax.axis_size("local") // SHARDS)
    count, wide = tokens.shape
    depth, hidden = gate_proj.shape[1:]
    subs = wide // LANES
    weights = (SCALE * scores / jnp.sum(scores, axis=1, keepdims=True)).astype(jnp.bfloat16).astype(jnp.float32)
    labels = jnp.arange(plane, dtype=jnp.int32)
    matches = routes[:, :, None] == labels[None, None, :]
    named = jnp.any(matches, axis=1)
    earlier = jnp.arange(count)[:, None] > jnp.arange(count)[None, :]
    rank = jnp.sum(earlier[:, :, None] & named[None], axis=1, dtype=jnp.int32)
    slots = jnp.arange(MOST, dtype=jnp.int32)
    chosen = named[None] & (rank[None] == slots[:, None, None])
    pick = jnp.sum(jnp.where(chosen, jnp.arange(count, dtype=jnp.int32)[None, :, None], 0), axis=1)
    home = jnp.sum(jnp.where(matches, rank[:, None, :] * plane + labels[None, None, :], 0), axis=2)
    bf16, f32 = jnp.bfloat16, jnp.float32
    dma = pltpu.SemaphoreType.DMA
    vmem, smem, hbm = pltpu.VMEM, pltpu.SMEM, pl.ANY
    out = pl.pallas_call(
        functools.partial(kernel, plane, MOST, wide),
        out_shape=jax.ShapeDtypeStruct((count, subs, LANES), bf16),
        in_specs=[pl.BlockSpec(memory_space=m) for m in (smem, smem, smem, vmem, hbm, hbm, hbm)],
        out_specs=pl.BlockSpec(memory_space=vmem),
        scratch_shapes=[
            vmem((depth, hidden), bf16),
            vmem((depth, hidden), bf16),
            vmem((hidden, depth), bf16),
            vmem((MOST, plane, subs, LANES), bf16),
            vmem((MOST, plane, subs, LANES), bf16),
            vmem((MOST, SHARDS, plane, wide), bf16),
            vmem((MOST, SHARDS, plane, wide), bf16),
            vmem((MOST, 2, plane // 2, wide), bf16),
            vmem((MOST, 2, plane, wide), bf16),
            vmem((MOST, plane, subs, LANES), bf16),
            vmem((MOST, plane, subs, LANES), bf16),
            vmem((plane * subs, LANES), f32),
            vmem((SHARDS * plane, 2 * hidden), f32),
            vmem((SHARDS * plane, hidden), bf16),
            dma((3,)),
            dma((MOST,)), dma((MOST,)),
            dma((MOST, 2)), dma((MOST, 2)),
            dma((MOST, 2)), dma((MOST, 2)),
            dma((MOST, 2)), dma((MOST, 2)),
            dma((MOST, 2)), dma((MOST, 2)),
            dma((MOST,)), dma((MOST,)),
        ],
        compiler_params=pltpu.CompilerParams(
            collective_id=0, has_side_effects=True, vmem_limit_bytes=67043328
        ),
    )(pick, home, weights, tokens.reshape(count, subs, LANES), gate_proj, up_proj, down_proj)
    return out.reshape(count, wide)


def solution(mesh):
    both = ("node", "local")
    return jax.shard_map(
        per_device,
        mesh=mesh,
        in_specs=(P(both, None),) * 3 + (P(both, None, None),) * 3,
        out_specs=P(both, None),
        check_vma=False,
    )
```

time: 524 us -> 195 us (0.37)
  waiting for transfers between devices: 209 us -> 0 us
  Pallas kernels: 0 us -> 183 us
  blocking collectives: 110 us -> 0 us
  local copies, waits for them, and re-layouts: 108 us -> 6.04 us
  other arithmetic: 44.2 us -> 4.74 us
  starting transfers between devices: 25.9 us -> 0 us
  matrix products: 23.4 us -> 0 us
    all_to_all x4 -> x0, waiting for transfers between devices: 209 us -> none  [the longest x1 143 us: per_device(): lax.all_to_all(results, 'local', split_axis=0, concat_axis=0, tiled=True)]
    pallas_call x0 -> x1, Pallas kernels: none -> 183 us  [per_device(): pl.pallas_call(functools.partial(kernel, plane, MOST, wide), out_shape=ja...]
    all_to_all x1 -> x0, blocking collectives: 110 us -> none  [per_device(): lax.all_to_all(outgoing, 'local', split_axis=0, concat_axis=0, tiled=True)]
    gather x3 -> x0, local copies, waits for them, and re-layouts: 95.9 us -> none  [the longest x2 67.3 us: per_device(): gathered = summed[local_ids[None, :], jnp.clip(position, 0, capacity - 1)]]
    reduce_sum x4 -> x3, other arithmetic: 35.9 us -> 2.65 us  [the longest x1 1.16 us: per_device(): rank = jnp.sum(earlier[:, :, None] & named[None], axis=1, dtype=jnp.int32)]
    all_to_all x4 -> x0, starting transfers between devices: 25.9 us -> none  [the longest x1 10.1 us: per_device(): lax.all_to_all(node_total.astype(jnp.bfloat16), 'node', split_axis=0, con...]
    dot_general x6 -> x0, matrix products: 23.4 us -> none  [the longest x1 7.44 us: expert_block(): gate_act = jnp.dot(flat_rows, w_gate, preferred_element_type=jnp.float32)]
  transfers between devices with their start and end apart: 4 -> 0, of which waited for: 4 -> 0; matrix products, arithmetic and copies ran while one was open for 1% -> 0% of each run, Pallas kernels for 0% -> 0%
where the time goes in v1:
time: 195 us; the launch traced here: 194 us
  Pallas kernels  183 us (94%)
  local copies, waits for them, and re-layouts  6.04 us (3%)
  other arithmetic  4.74 us (2%)
    pallas_call x1, Pallas kernels, per_device(): pl.pallas_call(functools.partial(kernel, plane, MOST, wide), out_shape=ja...  183 us
    unnamed x2, local copies, waits for them, and re-layouts  4.51 us

profile of v1, /device:TPU:1, one launch (start us, length us, event | category | flops | bytes accessed | tf_op | source)
XLA Modules:
  0.0 194.3 jit_solution(14935849713306904955)
XLA Ops:
  0.0 0.7 reduce_sum.39
  0.7 0.7 fusion.3
  1.4 0.7 fusion.1
  2.1 1.2 convert_reduce_fusion
  3.3 0.1 copy.17
  3.3 0.8 select_reduce_fusion.pick_ref
  4.1 0.1 copy.18
  4.2 0.7 select_reduce_fusion.1
  4.9 0.7 copy.19.home_ref
  5.6 0.7 copy.20.weight_ref
  6.3 2.3 %copy.21 = bf16[8,8,56,128]{3,2,1,0:T(8,128)(2,1)} copy(bf16[8,8,56,128]{3,1,2,0:T(8,128)(2,1)} %bitcast.8) | data formatting | bytes 1835008
  8.6 183.5 %shard_map.64 = bf16[64,56,128]{2,1,0:T(8,128)(2,1)} custom-call(s32[5,32]{1,0:T(8,128)} %select_reduce_fusion.pick_ref, s32[64,2]{1,0:T(8,128)} %copy.19.home_ref, f32[64,2]{1,0:T(8,128)} %copy.20.weight_ref, bf16[64,56,128]{2,1,0:T(8,128)(2,1)} %bitcast.7, bf16[1,7168,512]{2,1,0:T(8,128)(2,1)} %gate_hbm.1, bf16[1,7168,512]{2,1,0:T(8,128)(2,1)} %up_hbm.1, ...), custom_call_target="tpu_custom_call" | custom-call | tf_op jit(solution)/shard_map/pallas_call | solution.py:269
  192.1 2.3 %copy.24 = bf16[8,8,56,128]{3,1,2,0:T(8,128)(2,1)} copy(bf16[8,8,56,128]{3,2,1,0:T(8,128)(2,1)} %bitcast.6) | data formatting | bytes 1835008
  (2 shorter events, 0.0 us)

commit v2 on v1

v2 whole, which is shorter than its diff:
```python
import functools

import jax
import jax.numpy as jnp
from jax import lax
from jax.experimental import pallas as pl
from jax.experimental.pallas import tpu as pltpu
from jax.sharding import PartitionSpec as P

MESH = pl.DeviceIdType.MESH
SHARDS = 4
SCALE = 2.827
MOST = 5
LANES = 128
LATE_IN = 2
LATE_OUT = 2
PARTS = 7
f32, bf16 = jnp.float32, jnp.bfloat16


def kernel(
    plane, count, block,
    itab_own, itab_in, ftab_in, tok_a, tok_b, gate_hbm, up_hbm, down_hbm,
    out_ref,
    w_gate, w_up, w_down, itab_v, ftab_v, itab, ftab, tok_all, sent_a, sent_b, got_a, got_b, x_a, x_b, part,
    half_in, full_in, back_a, back_b, home_a, home_b, mix, mix_half, mix_full, wide32, acc, hid,
    w_sem, tab_s, tab_r, tab_l, tok_s, tok_r, tfw_s, tfw_r, pa_s, pa_r, pb_s, pb_r, ag_s, ag_r, fw_s, fw_r,
    rh_s, rh_r, rf_s, rf_r, ba_s, ba_r, bb_s, bb_r, mh_s, mh_r, mf_s, mf_r,
):
    node, local = lax.axis_index("node"), lax.axis_index("local")
    ys = lax.axis_size("local") // SHARDS
    y, z = local // SHARDS, local % SHARDS
    me = node * ys + y
    nxt, far, prv = [(z + d) % SHARDS for d in (1, 2, 3)]
    nxt_dev, far_dev, prv_dev = [(node, y * SHARDS + q) for q in (nxt, far, prv)]
    z_devs = (nxt_dev, far_dev, prv_dev)
    hidden = w_gate.shape[1]
    step_subs = block // LANES
    in_a, in_b = (PARTS - LATE_IN) * step_subs, LATE_IN * step_subs
    out_a, out_b = (PARTS - LATE_OUT) * step_subs, LATE_OUT * step_subs
    half, half_t = plane // 2, count // 2
    rows = SHARDS * plane
    low, high = pl.ds(0, half), pl.ds(half, half)

    def loop(n, body, start=0, unroll=1):
        def wrapped(i, carry):
            body(i)
            return carry

        lax.fori_loop(start, n, wrapped, 0, unroll=unroll)

    w_copies = [
        pltpu.make_async_copy(gate_hbm.at[0], w_gate, w_sem.at[0]),
        pltpu.make_async_copy(up_hbm.at[0], w_up, w_sem.at[1]),
        pltpu.make_async_copy(down_hbm.at[0], w_down, w_sem.at[2]),
    ]
    for copy in w_copies:
        copy.start()

    def peer(k):
        other = lax.rem(me + k, plane)
        return other, (other // ys, (other % ys) * SHARDS + z)

    barrier = pltpu.get_barrier_semaphore()

    @functools.partial(loop, plane, start=1)
    def _(k):
        pl.semaphore_signal(barrier, inc=1, device_id=peer(k)[1], device_id_type=MESH)

    for dev in z_devs:
        pl.semaphore_signal(barrier, inc=1, device_id=dev, device_id_type=MESH)

    def remote(src, dst, s_sem, r_sem, dev):
        return pltpu.make_async_remote_copy(
            src_ref=src, dst_ref=dst, send_sem=s_sem, recv_sem=r_sem, device_id=dev, device_id_type=MESH
        )

    def spread(src, dst, s_sem, r_sem, c):
        @functools.partial(loop, plane, start=1)
        def _(k):
            other, dev = peer(k)
            remote(src.at[c, other], dst.at[c, me], s_sem.at[c], r_sem.at[c], dev).start()

        dst[c, me] = src[c, me]

    def spread_all(src, dst, s_sem, r_sem, c):
        some = pl.ds(0, plane - 1)
        return remote(src.at[c, some], dst.at[c, some], s_sem.at[c], r_sem.at[c], nxt_dev)

    plane_a = functools.partial(spread_all, sent_a, got_a, pa_s, pa_r)
    plane_b = functools.partial(spread_all, sent_b, got_b, pb_s, pb_r)
    return_a = functools.partial(spread_all, back_a, home_a, ba_s, ba_r)
    return_b = functools.partial(spread_all, back_b, home_b, bb_s, bb_r)

    def tables():
        copies = []
        for d, dev in enumerate(z_devs):
            copies.append(remote(itab_in, itab_v.at[z], tab_s.at[d, 0], tab_r.at[d, 0], dev))
            copies.append(remote(ftab_in, ftab_v.at[z], tab_s.at[d, 1], tab_r.at[d, 1], dev))
        return copies

    def gather_tokens():
        return (
            remote(tok_b, tok_all.at[z], tok_s.at[0], tok_r.at[0], nxt_dev),
            remote(tok_b, tok_all.at[z], tok_s.at[1], tok_r.at[1], prv_dev),
        )

    def forward_tokens():
        first, second = pl.ds(0, half_t), pl.ds(half_t, half_t)
        return (
            remote(tok_all.at[prv, first], tok_all.at[prv, first], tfw_s.at[0], tfw_r.at[0], nxt_dev),
            remote(tok_all.at[nxt, second], tok_all.at[nxt, second], tfw_s.at[1], tfw_r.at[1], prv_dev),
        )

    def gather(c):
        return (
            remote(x_a.at[c, z], x_a.at[c, z], ag_s.at[c, 0], ag_r.at[c, 0], nxt_dev),
            remote(x_a.at[c, z], x_a.at[c, z], ag_s.at[c, 1], ag_r.at[c, 1], prv_dev),
        )

    def forward(c):
        return (
            remote(x_a.at[c, prv, low], x_a.at[c, prv, low], fw_s.at[c, 0], fw_r.at[c, 0], nxt_dev),
            remote(x_a.at[c, nxt, high], x_a.at[c, nxt, high], fw_s.at[c, 1], fw_r.at[c, 1], prv_dev),
        )

    def scatter_half(c):
        return (
            remote(part.at[c, far, low], half_in.at[c, 0], rh_s.at[c, 0], rh_r.at[c, 0], nxt_dev),
            remote(part.at[c, far, high], half_in.at[c, 1], rh_s.at[c, 1], rh_r.at[c, 1], prv_dev),
        )

    def scatter_full(c):
        return (
            remote(part.at[c, nxt], full_in.at[c, 0], rf_s.at[c, 0], rf_r.at[c, 0], nxt_dev),
            remote(part.at[c, prv], full_in.at[c, 1], rf_s.at[c, 1], rf_r.at[c, 1], prv_dev),
        )

    def mix_halves():
        first, second = pl.ds(0, half_t), pl.ds(half_t, half_t)
        return (
            remote(mix.at[far, first], mix_half.at[0], mh_s.at[0], mh_r.at[0], nxt_dev),
            remote(mix.at[far, second], mix_half.at[1], mh_s.at[1], mh_r.at[1], prv_dev),
        )

    def mix_fulls():
        return (
            remote(mix.at[nxt], mix_full.at[0], mf_s.at[0], mf_r.at[0], nxt_dev),
            remote(mix.at[prv], mix_full.at[1], mf_s.at[1], mf_r.at[1], prv_dev),
        )

    def launch_a(c):
        @functools.partial(loop, plane)
        def _(e):
            sent_a[c, e] = tok_a[itab_own[c // 4, (c % 4) * plane + e]]

        spread(sent_a, got_a, pa_s, pa_r, c)

    def launch_b(c):
        @functools.partial(loop, plane)
        def _(e):
            for q in range(SHARDS):
                sent_b[c, e, q] = tok_all[q, itab[q, c // 4, (c % 4) * plane + e]]

        spread(sent_b, got_b, pb_s, pb_r, c)

    def stage_a(c):
        plane_a(c).wait_recv()

        @functools.partial(loop, plane)
        def _(s):
            wide32[pl.ds(pl.multiple_of(s * in_a, 8), in_a), :] = got_a[c, s].astype(f32)

        @functools.partial(loop, in_a)
        def _(j):
            cols = pl.ds(pl.multiple_of(j * LANES, LANES), LANES)
            for s0 in range(0, plane, 16):
                pair = [wide32[pl.ds((s0 + d) * in_a + j, 8, stride=in_a), :] for d in (0, 8)]
                x_a[c, z, pl.ds(s0, 16), cols] = jnp.concatenate(pair, axis=0).astype(bf16)

        for copy in gather(c):
            copy.start()

    def stage_b(c):
        for copy in gather(c):
            copy.wait_recv()
        for copy in forward(c):
            copy.start()

    def stage_c(c):
        plane_b(c).wait_recv()

        @functools.partial(loop, plane)
        def _(p):
            for q in range(SHARDS):
                wide32[pl.ds(pl.multiple_of((q * plane + p) * in_b, 8), in_b), :] = got_b[c, p, q].astype(f32)

        @functools.partial(loop, in_b)
        def _(j):
            cols = pl.ds(pl.multiple_of(j * LANES, LANES), LANES)
            for s0 in range(0, rows, 16):
                pair = [wide32[pl.ds((s0 + d) * in_b + j, 8, stride=in_b), :] for d in (0, 8)]
                x_b[pl.ds(s0, 16), cols] = jnp.concatenate(pair, axis=0).astype(bf16)

        acc[...] = jnp.zeros_like(acc)

        def contract(rows_k, span):
            acc[:, :hidden] += jnp.dot(rows_k, w_gate[span, :], preferred_element_type=f32)
            acc[:, hidden:] += jnp.dot(rows_k, w_up[span, :], preferred_element_type=f32)

        @functools.partial(loop, LATE_IN)
        def _(k):
            here = pl.ds(pl.multiple_of(k * block, LANES), block)
            contract(x_b[:, here], pl.ds(pl.multiple_of((PARTS - LATE_IN + k) * block, LANES), block))

        for copy in forward(c):
            copy.wait_recv()

        @functools.partial(loop, PARTS - LATE_IN)
        def _(k):
            here = pl.ds(pl.multiple_of(k * block, LANES), block)
            contract(x_a[c, :, :, here].reshape(rows, block), here)

        gate = acc[:, :hidden]
        hid[...] = (gate / (1.0 + jnp.exp(-gate)) * acc[:, hidden:]).astype(bf16)

        @functools.partial(loop, PARTS - LATE_OUT)
        def _(k):
            span = pl.ds(pl.multiple_of(k * block, LANES), block)
            value = jnp.dot(hid[...], w_down[:, span], preferred_element_type=f32)
            part[c, :, :, span] = value.astype(bf16).reshape(SHARDS, plane, block)

        for copy in scatter_half(c):
            copy.start()

        @functools.partial(loop, LATE_OUT)
        def _(k):
            span = pl.ds(pl.multiple_of((PARTS - LATE_OUT + k) * block, LANES), block)
            value = jnp.dot(hid[...], w_down[:, span], preferred_element_type=f32)
            for j in range(step_subs):
                for s0 in range(0, rows, 8):
                    wide32[pl.ds(s0 * out_b + k * step_subs + j, 8, stride=out_b), :] = (
                        value[s0:s0 + 8, j * LANES:(j + 1) * LANES]
                    )

        @functools.partial(loop, plane)
        def _(p):
            for q in range(SHARDS):
                span = pl.ds(pl.multiple_of((q * plane + p) * out_b, 8), out_b)
                back_b[c, p, q] = wide32[span, :].astype(bf16)

        spread(back_b, home_b, bb_s, bb_r, c)

    def stage_e(c):
        for copy in scatter_half(c):
            copy.wait_recv()
        for side, owner, span in ((0, nxt, low), (1, prv, high)):
            mine = part[c, owner, span].astype(f32)
            part[c, owner, span] = (mine + half_in[c, side].astype(f32)).astype(bf16)
        for copy in scatter_full(c):
            copy.start()

    def stage_f(c):
        for copy in scatter_full(c):
            copy.wait_recv()

        @functools.partial(loop, out_a)
        def _(j):
            cols = pl.ds(pl.multiple_of(j * LANES, LANES), LANES)
            for s0 in range(0, plane, 16):
                span = pl.ds(s0, 16)
                value = part[c, z, span, cols].astype(f32)
                value = value + full_in[c, 0, span, cols].astype(f32)
                value = value + full_in[c, 1, span, cols].astype(f32)
                for d in (0, 8):
                    wide32[pl.ds((s0 + d) * out_a + j, 8, stride=out_a), :] = value[d:d + 8]

        @functools.partial(loop, plane)
        def _(s):
            back_a[c, s] = wide32[pl.ds(pl.multiple_of(s * out_a, 8), out_a), :].astype(bf16)

        spread(back_a, home_a, ba_s, ba_r, c)

    def weighted(source, q, t, subs, pick):
        total = jnp.zeros((subs, LANES), f32)
        for k in range(2):
            spot = itab[q, 2, t * 2 + k]
            total = total + ftab[q, 0, t * 2 + k] * pick(source, spot // plane, spot % plane)
        return total

    def mix_one(q):
        @functools.partial(loop, count)
        def _(t):
            take = lambda ref, c, e: ref[c, e, q].astype(f32)
            mix[q, t] = weighted(home_b, q, t, out_b, take).astype(bf16)

    pl.semaphore_wait(barrier, plane + 2)
    for copy in gather_tokens():
        copy.start()
    for copy in tables():
        copy.start()
    tok_all[z] = tok_b[...]
    loop(3, launch_a)
    for copy in gather_tokens():
        copy.wait_recv()
    for copy in forward_tokens():
        copy.start()

    def ready():
        for copy in tables():
            copy.wait_recv()
        moves = [
            pltpu.make_async_copy(itab_in, itab.at[z], tab_l.at[0]),
            pltpu.make_async_copy(ftab_in, ftab.at[z], tab_l.at[1]),
        ]
        for d, q in enumerate((nxt, far, prv)):
            moves.append(pltpu.make_async_copy(itab_v.at[q], itab.at[q], tab_l.at[2 + 2 * d]))
            moves.append(pltpu.make_async_copy(ftab_v.at[q], ftab.at[q], tab_l.at[3 + 2 * d]))
        for move in moves:
            move.start()
        for move in moves:
            move.wait()
        for copy in forward_tokens():
            copy.wait_recv()
        for copy in w_copies:
            copy.wait()

    def late(c):
        launch_b(c)

        @pl.when(c + 3 < MOST)
        def _():
            launch_a(c + 3)

    stages = ((stage_a, 0), (late, 1), (stage_b, 1), (stage_c, 2), (stage_e, 3), (stage_f, 4))

    def run(s, skip_last=False):
        @pl.when(s == 1)
        def _():
            ready()

        for stage, lag in stages:
            c = s - lag

            @pl.when((c >= 0) & (c < MOST))
            def _(stage=stage, c=c):
                stage(c)

    loop(MOST + 3, run)

    @functools.partial(loop, MOST)
    def _(c):
        return_b(c).wait_recv()

    mix_one(far)
    for copy in mix_halves():
        copy.start()
    mix_one(nxt)
    mix_one(prv)
    mix_one(z)
    stage_f(MOST - 1)
    for copy in mix_halves():
        copy.wait_recv()
    for side, owner, start in ((0, nxt, 0), (1, prv, half_t)):
        @functools.partial(loop, half_t)
        def _(t):
            mix[owner, start + t] = (mix[owner, start + t].astype(f32) + mix_half[side, t].astype(f32)).astype(bf16)

    for copy in mix_fulls():
        copy.start()

    @functools.partial(loop, MOST)
    def _(c):
        return_a(c).wait_recv()

    @functools.partial(loop, count)
    def _(t):
        take = lambda ref, c, e: ref[c, e].astype(f32)
        out_ref[t, pl.ds(0, out_a)] = weighted(home_a, z, t, out_a, take).astype(bf16)

    for copy in mix_fulls():
        copy.wait_recv()

    @functools.partial(loop, count)
    def _(t):
        total = mix[z, t].astype(f32) + mix_full[0, t].astype(f32) + mix_full[1, t].astype(f32)
        out_ref[t, pl.ds(out_a, out_b)] = total.astype(bf16)

    for copy in (*tables(), *gather_tokens(), *forward_tokens(), *mix_halves(), *mix_fulls()):
        copy.wait_send()

    @functools.partial(loop, MOST)
    def _(c):
        for copy in (plane_a(c), plane_b(c), return_a(c), return_b(c)):
            copy.wait_send()
        for group in (gather, forward, scatter_half, scatter_full):
            for copy in group(c):
                copy.wait_send()


def per_device(tokens, routes, scores, gate_proj, up_proj, down_proj):
    plane = lax.axis_size("node") * (lax.axis_size("local") // SHARDS)
    count, wide = tokens.shape
    depth, hidden = gate_proj.shape[1:]
    block = wide // PARTS
    subs, step_subs = wide // LANES, block // LANES
    weights = (SCALE * scores / jnp.sum(scores, axis=1, keepdims=True)).astype(bf16).astype(f32)
    labels = jnp.arange(plane, dtype=jnp.int32)
    matches = routes[:, :, None] == labels[None, None, :]
    named = jnp.any(matches, axis=1)
    earlier = jnp.arange(count)[:, None] > jnp.arange(count)[None, :]
    rank = jnp.sum(earlier[:, :, None] & named[None], axis=1, dtype=jnp.int32)
    slots = jnp.arange(8, dtype=jnp.int32)
    chosen = named[None] & (rank[None] == slots[:, None, None]) & (slots < MOST)[:, None, None]
    pick = jnp.sum(jnp.where(chosen, jnp.arange(count, dtype=jnp.int32)[None, :, None], 0), axis=1)
    home = jnp.sum(jnp.where(matches, rank[:, None, :] * plane + labels[None, None, :], 0), axis=2)
    itab = jnp.zeros((8, LANES), jnp.int32)
    itab = itab.at[:2, :4 * plane].set(pick.reshape(2, 4 * plane)).at[2, :2 * count].set(home.reshape(-1))
    ftab = jnp.zeros((8, LANES), f32).at[0, :2 * count].set(weights.reshape(-1))
    in_a, in_b = (PARTS - LATE_IN) * step_subs, LATE_IN * step_subs
    out_a, out_b = (PARTS - LATE_OUT) * step_subs, LATE_OUT * step_subs
    tok = tokens.reshape(count, subs, LANES)
    dma = pltpu.SemaphoreType.DMA
    vmem, smem, hbm = pltpu.VMEM, pltpu.SMEM, pl.ANY
    sent_b = vmem((MOST, plane, SHARDS, in_b, LANES), bf16)
    out = pl.pallas_call(
        functools.partial(kernel, plane, count, block),
        out_shape=jax.ShapeDtypeStruct((count, subs, LANES), bf16),
        in_specs=[pl.BlockSpec(memory_space=m) for m in (smem, vmem, vmem, vmem, vmem, hbm, hbm, hbm)],
        out_specs=pl.BlockSpec(memory_space=vmem),
        scratch_shapes=[
            vmem((depth, hidden), bf16),
            vmem((depth, hidden), bf16),
            vmem((hidden, depth), bf16),
            vmem((SHARDS, 8, LANES), jnp.int32),
            vmem((SHARDS, 8, LANES), f32),
            smem((SHARDS, 8, LANES), jnp.int32),
            smem((SHARDS, 8, LANES), f32),
            vmem((SHARDS, count, in_b, LANES), bf16),
            vmem((MOST, plane, in_a, LANES), bf16),
            vmem((MOST, plane, SHARDS, in_b, LANES), bf16),
            vmem((MOST, plane, in_a, LANES), bf16),
            vmem((MOST, plane, SHARDS, in_b, LANES), bf16),
            vmem((MOST, SHARDS, plane, in_a * LANES), bf16),
            vmem((SHARDS * plane, in_b * LANES), bf16),
            vmem((MOST, SHARDS, plane, out_a * LANES), bf16),
            vmem((MOST, 2, plane // 2, out_a * LANES), bf16),
            vmem((MOST, 2, plane, out_a * LANES), bf16),
            vmem((MOST, plane, out_a, LANES), bf16),
            vmem((MOST, plane, SHARDS, out_b, LANES), bf16),
            vmem((MOST, plane, out_a, LANES), bf16),
            vmem((MOST, plane, SHARDS, out_b, LANES), bf16),
            vmem((SHARDS, count, out_b, LANES), bf16),
            vmem((2, count // 2, out_b, LANES), bf16),
            vmem((2, count, out_b, LANES), bf16),
            vmem((plane * max(in_a, out_a, SHARDS * in_b, SHARDS * out_b), LANES), f32),
            vmem((SHARDS * plane, 2 * hidden), f32),
            vmem((SHARDS * plane, hidden), bf16),
            dma((3,)),
            dma((3, 2)), dma((3, 2)), dma((8,)),
            dma((2,)), dma((2,)),
            dma((2,)), dma((2,)),
            dma((MOST,)), dma((MOST,)),
            dma((MOST,)), dma((MOST,)),
            dma((MOST, 2)), dma((MOST, 2)),
            dma((MOST, 2)), dma((MOST, 2)),
            dma((MOST, 2)), dma((MOST, 2)),
            dma((MOST, 2)), dma((MOST, 2)),
            dma((MOST,)), dma((MOST,)),
            dma((MOST,)), dma((MOST,)),
            dma((2,)), dma((2,)),
            dma((2,)), dma((2,)),
        ],
        compiler_params=pltpu.CompilerParams(
            collective_id=0, has_side_effects=True, vmem_limit_bytes=67043328
        ),
    )(itab, itab, ftab, tok[:, :in_a], tok[:, in_a:], gate_proj, up_proj, down_proj)
    return out.reshape(count, wide)


def solution(mesh):
    both = ("node", "local")
    return jax.shard_map(
        per_device,
        mesh=mesh,
        in_specs=(P(both, None),) * 3 + (P(both, None, None),) * 3,
        out_specs=P(both, None),
        check_vma=False,
    )
```

time: 195 us -> 155 us (0.79)
  Pallas kernels: 183 us -> 141 us
    pallas_call x1, Pallas kernels: 183 us -> 141 us  [per_device(): pl.pallas_call(functools.partial(kernel, plane, count, block), out_shape=...]
where the time goes in v2:
time: 155 us; the launch traced here: 154 us
  Pallas kernels  141 us (91%)
  local copies, waits for them, and re-layouts  7.76 us (5%)
  other arithmetic  4.86 us (3%)
    pallas_call x1, Pallas kernels, per_device(): pl.pallas_call(functools.partial(kernel, plane, count, block), out_shape=...  141 us
    unnamed x2, local copies, waits for them, and re-layouts  3.58 us

profile of v2, /device:TPU:1, one launch (start us, length us, event | category | flops | bytes accessed | tf_op | source)
XLA Modules:
  0.0 154.2 jit_solution(6810658381040632106)
XLA Ops:
  0.0 0.7 reduce_sum.39
  0.7 0.7 fusion.3
  1.4 0.7 fusion.2
  2.1 0.1 copy.14
  2.2 0.1 reshape.121
  2.4 0.6 pad_convert_fusion.ftab_in
  3.0 1.2 convert_reduce_fusion
  4.1 0.1 copy.11
  4.2 0.3 select_reduce_fusion
  4.5 0.1 reshape.119
  4.6 0.1 copy.12
  4.6 0.7 select_reduce_fusion.1
  5.4 0.6 scatter.14
  6.0 0.1 copy.13
  6.1 0.1 reshape.120
  6.2 1.3 scatter.18.itab_own.itab_in
  7.5 1.3 copy.15
  8.8 0.7 slice.54.tok_b
  9.5 0.9 slice.53.tok_a
  10.4 141.5 %shard_map.64 = bf16[64,56,128]{2,1,0:T(8,128)(2,1)} custom-call(s32[8,128]{1,0:T(8,128)} %scatter.18.itab_own.itab_in, s32[8,128]{1,0:T(8,128)} %scatter.18.itab_own.itab_in, f32[8,128]{1,0:T(8,128)} %pad_convert_fusion.ftab_in, bf16[64,40,128]{2,1,0:T(8,128)(2,1)} %slice.53.tok_a, bf16[64,16,128]{2,1,0:T(8,128)(2,1)} %slice.54.tok_b, ...), custom_call_target="tpu_custom_call" | custom-call | tf_op jit(solution)/shard_map/pallas_call | solution.py:426
  151.9 2.3 %copy.18 = bf16[8,8,56,128]{3,1,2,0:T(8,128)(2,1)} copy(bf16[8,8,56,128]{3,2,1,0:T(8,128)(2,1)} %bitcast.8) | data formatting | bytes 1835008
  (3 shorter events, 0.0 us)

commit v3 on v2

--- a/solution.py
+++ b/solution.py
@@ -13,16 +13,16 @@
 MOST = 5
 LANES = 128
 LATE_IN = 2
-LATE_OUT = 2
+LATE_OUT = 3
 PARTS = 7
 f32, bf16 = jnp.float32, jnp.bfloat16
 
 
 def kernel(
     plane, count, block,
-    itab_own, itab_in, ftab_in, tok_a, tok_b, gate_hbm, up_hbm, down_hbm,
+    routes_ref, scores_ref, tok_ref, gate_hbm, up_hbm, down_hbm,
     out_ref,
-    w_gate, w_up, w_down, itab_v, ftab_v, itab, ftab, tok_all, sent_a, sent_b, got_a, got_b, x_a, x_b, part,
+    w_gate, w_up, w_down, itab_in, ftab_in, itab_v, ftab_v, itab, ftab, tok_all, tok_a, sent_a, sent_b, got_a, got_b, x_a, x_b, part,
     half_in, full_in, back_a, back_b, home_a, home_b, mix, mix_half, mix_full, wide32, acc, hid,
     w_sem, tab_s, tab_r, tab_l, tok_s, tok_r, tfw_s, tfw_r, pa_s, pa_r, pb_s, pb_r, ag_s, ag_r, fw_s, fw_r,
     rh_s, rh_r, rf_s, rf_r, ba_s, ba_r, bb_s, bb_r, mh_s, mh_r, mf_s, mf_r,
@@ -36,6 +36,7 @@
     z_devs = (nxt_dev, far_dev, prv_dev)
     hidden = w_gate.shape[1]
     step_subs = block // LANES
+    subs = PARTS * step_subs
     in_a, in_b = (PARTS - LATE_IN) * step_subs, LATE_IN * step_subs
     out_a, out_b = (PARTS - LATE_OUT) * step_subs, LATE_OUT * step_subs
     half, half_t = plane // 2, count // 2
@@ -101,8 +102,8 @@
 
     def gather_tokens():
         return (
-            remote(tok_b, tok_all.at[z], tok_s.at[0], tok_r.at[0], nxt_dev),
-            remote(tok_b, tok_all.at[z], tok_s.at[1], tok_r.at[1], prv_dev),
+            remote(tok_all.at[z], tok_all.at[z], tok_s.at[0], tok_r.at[0], nxt_dev),
+            remote(tok_all.at[z], tok_all.at[z], tok_s.at[1], tok_r.at[1], prv_dev),
         )
 
     def forward_tokens():
@@ -149,11 +150,12 @@
             remote(mix.at[prv], mix_full.at[1], mf_s.at[1], mf_r.at[1], prv_dev),
         )
 
-    def launch_a(c):
+    def fill_a(c):
         @functools.partial(loop, plane)
         def _(e):
-            sent_a[c, e] = tok_a[itab_own[c // 4, (c % 4) * plane + e]]
-
+            sent_a[c, e] = tok_a[itab[z, c // 4, (c % 4) * plane + e]]
+
+    def launch_a(c):
         spread(sent_a, got_a, pa_s, pa_r, c)
 
     def launch_b(c):
@@ -284,8 +286,8 @@
     def weighted(source, q, t, subs, pick):
         total = jnp.zeros((subs, LANES), f32)
         for k in range(2):
-            spot = itab[q, 2, t * 2 + k]
-            total = total + ftab[q, 0, t * 2 + k] * pick(source, spot // plane, spot % plane)
+            spot = itab[q, 2 + k, t]
+            total = total + ftab[q, k, t] * pick(source, spot // plane, spot % plane)
         return total
 
     def mix_one(q):
@@ -294,13 +296,67 @@
             take = lambda ref, c, e: ref[c, e, q].astype(f32)
             mix[q, t] = weighted(home_b, q, t, out_b, take).astype(bf16)
 
+    def own_tables():
+        routes, scores = routes_ref[...], scores_ref[...]
+        expert = lax.broadcasted_iota(jnp.int32, (plane, count), 0)
+        firsts, seconds = expert == routes[0:1, :], expert == routes[1:2, :]
+        named = jnp.where(firsts | seconds, 1, 0)
+        token = lax.broadcasted_iota(jnp.int32, (plane, count), 1)
+        rank = jnp.zeros((plane, count), jnp.int32)
+        for t in range(count - 1):
+            rank = rank + jnp.where(token > t, named[:, t:t + 1], 0)
+        spot = jnp.minimum(rank, MOST - 1) * plane + expert
+        itab_in[...] = jnp.zeros_like(itab_in)
+        ftab_in[...] = jnp.zeros_like(ftab_in)
+        lane = lax.broadcasted_iota(jnp.int32, (plane, LANES), 1)
+        sub = lax.broadcasted_iota(jnp.int32, (plane, LANES), 0)
+        for row, slots in ((0, range(4)), (1, range(4, MOST))):
+            spread_out = jnp.zeros((plane, LANES), jnp.int32)
+            for c in slots:
+                pick = jnp.sum(jnp.where(rank == c, named * token, 0), axis=1, keepdims=True)
+                spread_out = spread_out + jnp.where(lane == sub + (c % 4) * plane, pick, 0)
+            itab_in[row:row + 1, :] = jnp.sum(spread_out, axis=0, keepdims=True)
+        weights = (SCALE * scores / (scores[0:1, :] + scores[1:2, :])).astype(bf16).astype(f32)
+        for k, match in enumerate((firsts, seconds)):
+            where = jnp.sum(jnp.where(match, spot, 0), axis=0, keepdims=True)
+            itab_in[2 + k:3 + k, 0:count] = where
+            ftab_in[k:k + 1, 0:count] = weights[k:k + 1, :]
+
+    own_tables()
+
+    @functools.partial(loop, subs)
+    def _(j):
+        cols = pl.ds(pl.multiple_of(j * LANES, LANES), LANES)
+        for t0 in range(0, count, 16):
+            value = tok_ref[pl.ds(t0, 16), cols].astype(f32)
+            for d in (0, 8):
+                wide32[pl.ds((t0 + d) * subs + j, 8, stride=subs), :] = value[d:d + 8]
+
+    own_moves = [
+        pltpu.make_async_copy(itab_in, itab.at[z], tab_l.at[0]),
+        pltpu.make_async_copy(ftab_in, ftab.at[z], tab_l.at[1]),
+    ]
+    for move in own_moves:
+        move.start()
+
+    @functools.partial(loop, count)
+    def _(t):
+        tok_all[z, t] = wide32[pl.ds(pl.multiple_of(t * subs + in_a, 8), in_b), :].astype(bf16)
+        tok_a[t] = wide32[pl.ds(pl.multiple_of(t * subs, 8), in_a), :].astype(bf16)
+
+    for move in own_moves:
+        move.wait()
+    fill_a(0)
     pl.semaphore_wait(barrier, plane + 2)
     for copy in gather_tokens():
         copy.start()
     for copy in tables():
         copy.start()
-    tok_all[z] = tok_b[...]
-    loop(3, launch_a)
+    launch_a(0)
+    for c in range(1, MOST):
+        fill_a(c)
+        if c < 3:
+            launch_a(c)
     for copy in gather_tokens():
         copy.wait_recv()
     for copy in forward_tokens():
@@ -309,10 +365,7 @@
     def ready():
         for copy in tables():
             copy.wait_recv()
-        moves = [
-            pltpu.make_async_copy(itab_in, itab.at[z], tab_l.at[0]),
-            pltpu.make_async_copy(ftab_in, ftab.at[z], tab_l.at[1]),
-        ]
+        moves = []
         for d, q in enumerate((nxt, far, prv)):
             moves.append(pltpu.make_async_copy(itab_v.at[q], itab.at[q], tab_l.at[2 + 2 * d]))
             moves.append(pltpu.make_async_copy(ftab_v.at[q], ftab.at[q], tab_l.at[3 + 2 * d]))
@@ -376,16 +429,24 @@
     @functools.partial(loop, count)
     def _(t):
         take = lambda ref, c, e: ref[c, e].astype(f32)
-        out_ref[t, pl.ds(0, out_a)] = weighted(home_a, z, t, out_a, take).astype(bf16)
-
+        wide32[pl.ds(pl.multiple_of(t * subs, 8), out_a), :] = weighted(home_a, z, t, out_a, take)
+
+    def settle(j):
+        cols = pl.ds(pl.multiple_of(j * LANES, LANES), LANES)
+        for t0 in range(0, count, 16):
+            pair = [wide32[pl.ds((t0 + d) * subs + j, 8, stride=subs), :] for d in (0, 8)]
+            out_ref[pl.ds(t0, 16), cols] = jnp.concatenate(pair, axis=0).astype(bf16)
+
+    loop(out_a, settle)
     for copy in mix_fulls():
         copy.wait_recv()
 
     @functools.partial(loop, count)
     def _(t):
         total = mix[z, t].astype(f32) + mix_full[0, t].astype(f32) + mix_full[1, t].astype(f32)
-        out_ref[t, pl.ds(out_a, out_b)] = total.astype(bf16)
-
+        wide32[pl.ds(pl.multiple_of(t * subs + out_a, 8), out_b), :] = total
+
+    loop(subs, settle, start=out_a)
     for copy in (*tables(), *gather_tokens(), *forward_tokens(), *mix_halves(), *mix_fulls()):
         copy.wait_send()
 
@@ -404,39 +465,27 @@
     depth, hidden = gate_proj.shape[1:]
     block = wide // PARTS
     subs, step_subs = wide // LANES, block // LANES
-    weights = (SCALE * scores / jnp.sum(scores, axis=1, keepdims=True)).astype(bf16).astype(f32)
-    labels = jnp.arange(plane, dtype=jnp.int32)
-    matches = routes[:, :, None] == labels[None, None, :]
-    named = jnp.any(matches, axis=1)
-    earlier = jnp.arange(count)[:, None] > jnp.arange(count)[None, :]
-    rank = jnp.sum(earlier[:, :, None] & named[None], axis=1, dtype=jnp.int32)
-    slots = jnp.arange(8, dtype=jnp.int32)
-    chosen = named[None] & (rank[None] == slots[:, None, None]) & (slots < MOST)[:, None, None]
-    pick = jnp.sum(jnp.where(chosen, jnp.arange(count, dtype=jnp.int32)[None, :, None], 0), axis=1)
-    home = jnp.sum(jnp.where(matches, rank[:, None, :] * plane + labels[None, None, :], 0), axis=2)
-    itab = jnp.zeros((8, LANES), jnp.int32)
-    itab = itab.at[:2, :4 * plane].set(pick.reshape(2, 4 * plane)).at[2, :2 * count].set(home.reshape(-1))
-    ftab = jnp.zeros((8, LANES), f32).at[0, :2 * count].set(weights.reshape(-1))
     in_a, in_b = (PARTS - LATE_IN) * step_subs, LATE_IN * step_subs
     out_a, out_b = (PARTS - LATE_OUT) * step_subs, LATE_OUT * step_subs
-    tok = tokens.reshape(count, subs, LANES)
     dma = pltpu.SemaphoreType.DMA
     vmem, smem, hbm = pltpu.VMEM, pltpu.SMEM, pl.ANY
-    sent_b = vmem((MOST, plane, SHARDS, in_b, LANES), bf16)
-    out = pl.pallas_call(
+    return pl.pallas_call(
         functools.partial(kernel, plane, count, block),
-        out_shape=jax.ShapeDtypeStruct((count, subs, LANES), bf16),
-        in_specs=[pl.BlockSpec(memory_space=m) for m in (smem, vmem, vmem, vmem, vmem, hbm, hbm, hbm)],
+        out_shape=jax.ShapeDtypeStruct((count, wide), bf16),
+        in_specs=[pl.BlockSpec(memory_space=m) for m in (vmem, vmem, vmem, hbm, hbm, hbm)],
         out_specs=pl.BlockSpec(memory_space=vmem),
         scratch_shapes=[
             vmem((depth, hidden), bf16),
             vmem((depth, hidden), bf16),
             vmem((hidden, depth), bf16),
+            vmem((8, LANES), jnp.int32),
+            vmem((8, LANES), f32),
             vmem((SHARDS, 8, LANES), jnp.int32),
             vmem((SHARDS, 8, LANES), f32),
             smem((SHARDS, 8, LANES), jnp.int32),
             smem((SHARDS, 8, LANES), f32),
             vmem((SHARDS, count, in_b, LANES), bf16),
+            vmem((count, in_a, LANES), bf16),
             vmem((MOST, plane, in_a, LANES), bf16),
             vmem((MOST, plane, SHARDS, in_b, LANES), bf16),
             vmem((MOST, plane, in_a, LANES), bf16),
@@ -453,7 +502,7 @@
             vmem((SHARDS, count, out_b, LANES), bf16),
             vmem((2, count // 2, out_b, LANES), bf16),
             vmem((2, count, out_b, LANES), bf16),
-            vmem((plane * max(in_a, out_a, SHARDS * in_b, SHARDS * out_b), LANES), f32),
+            vmem((max(plane * max(in_a, out_a, SHARDS * in_b, SHARDS * out_b), count * subs), LANES), f32),
             vmem((SHARDS * plane, 2 * hidden), f32),
             vmem((SHARDS * plane, hidden), bf16),
             dma((3,)),
@@ -474,8 +523,7 @@
         compiler_params=pltpu.CompilerParams(
             collective_id=0, has_side_effects=True, vmem_limit_bytes=67043328
         ),
-    )(itab, itab, ftab, tok[:, :in_a], tok[:, in_a:], gate_proj, up_proj, down_proj)
-    return out.reshape(count, wide)
+    )(routes.T, scores.T, tokens, gate_proj, up_proj, down_proj)
 
 
 def solution(mesh):

time: 155 us -> 139 us (0.90)
  Pallas kernels: 141 us -> 135 us
  local copies, waits for them, and re-layouts: 7.76 us -> 2.16 us
  other arithmetic: 4.86 us -> 0 us
    pallas_call x1, Pallas kernels: 141 us -> 135 us  [per_device(): pl.pallas_call(functools.partial(kernel, plane, count, block), out_shape=...]
    reduce_sum x4 -> x0, other arithmetic: 2.86 us -> none  [the longest x1 1.16 us: per_device(): rank = jnp.sum(earlier[:, :, None] & named[None], axis=1, dtype=jnp.int32)]
    scatter x2 -> x0, local copies, waits for them, and re-layouts: 1.87 us -> none  [per_device(): itab.at[:2, :4 * plane].set(pick.reshape(2, 4 * plane)).at[2, :2 * count]]
    slice x2 -> x0, local copies, waits for them, and re-layouts: 1.6 us -> none  [the longest x1 0.89 us: per_device(): tok[:, :in_a]]
    unnamed x2 -> x1, local copies, waits for them, and re-layouts: 3.58 us -> 2.16 us
where the time goes in v3:
time: 139 us; the launch traced here: 137 us
  Pallas kernels  135 us (97%)
  local copies, waits for them, and re-layouts  2.16 us (2%)
    pallas_call x1, Pallas kernels, per_device(): pl.pallas_call(functools.partial(kernel, plane, count, block), out_shape=...  135 us

profile of v3, /device:TPU:1, one launch (start us, length us, event | category | flops | bytes accessed | tf_op | source)
XLA Modules:
  0.0 137.4 jit_solution(15086952602832365480)
XLA Ops:
  0.0 135.3 %shard_map.64 = bf16[64,7168]{1,0:T(8,128)(2,1)} custom-call(s32[2,64]{1,0:T(2,128)} %bitcast.2, f32[2,64]{1,0:T(2,128)} %bitcast.3, bf16[64,7168]{1,0:T(8,128)(2,1)} %tok_ref.1, bf16[1,7168,512]{2,1,0:T(8,128)(2,1)} %gate_hbm.1, bf16[1,7168,512]{2,1,0:T(8,128)(2,1)} %up_hbm.1, bf16[1,512,7168]{2,1,0:T(8,128)(2,1)} %down_hbm.1), custom_call_target="tpu_custom_call" | custom-call | tf_op jit(solution)/shard_map/pallas_call | solution.py:472
  135.3 2.2 %copy.8 = bf16[64,7168]{1,0:T(8,128)(2,1)} copy(bf16[64,7168]{1,0:T(8,128)(2,1)} %shard_map.64) | data formatting | bytes 1835008

commit v4 on v3

--- a/solution.py
+++ b/solution.py
@@ -15,6 +15,7 @@
 LATE_IN = 2
 LATE_OUT = 3
 PARTS = 7
+UNROLL = 4
 f32, bf16 = jnp.float32, jnp.bfloat16
 
 
@@ -43,7 +44,7 @@
     rows = SHARDS * plane
     low, high = pl.ds(0, half), pl.ds(half, half)
 
-    def loop(n, body, start=0, unroll=1):
+    def loop(n, body, start=0, unroll=UNROLL):
         def wrapped(i, carry):
             body(i)
             return carry
@@ -64,7 +65,7 @@
 
     barrier = pltpu.get_barrier_semaphore()
 
-    @functools.partial(loop, plane, start=1)
+    @functools.partial(loop, plane, start=1, unroll=plane - 1)
     def _(k):
         pl.semaphore_signal(barrier, inc=1, device_id=peer(k)[1], device_id_type=MESH)
 
@@ -77,7 +78,7 @@
         )
 
     def spread(src, dst, s_sem, r_sem, c):
-        @functools.partial(loop, plane, start=1)
+        @functools.partial(loop, plane, start=1, unroll=plane - 1)
         def _(k):
             other, dev = peer(k)
             remote(src.at[c, other], dst.at[c, me], s_sem.at[c], r_sem.at[c], dev).start()
@@ -100,55 +101,76 @@
             copies.append(remote(ftab_in, ftab_v.at[z], tab_s.at[d, 1], tab_r.at[d, 1], dev))
         return copies
 
-    def gather_tokens():
+    def both_ways(src_up, dst_up, src_dn, dst_dn, s_sem, r_sem):
         return (
-            remote(tok_all.at[z], tok_all.at[z], tok_s.at[0], tok_r.at[0], nxt_dev),
-            remote(tok_all.at[z], tok_all.at[z], tok_s.at[1], tok_r.at[1], prv_dev),
-        )
+            remote(src_up, dst_up, s_sem.at[0], r_sem.at[0], nxt_dev),
+            remote(src_dn, dst_dn, s_sem.at[1], r_sem.at[1], prv_dev),
+        )
+
+    def same(ref_up, ref_dn, s_sem, r_sem):
+        return both_ways(ref_up, ref_up, ref_dn, ref_dn, s_sem, r_sem)
+
+    first, second = pl.ds(0, half_t), pl.ds(half_t, half_t)
+
+    def lead_tokens():
+        return same(tok_all.at[z, first], tok_all.at[z, second], tok_s.at[0], tok_r.at[0])
+
+    def rest_tokens():
+        return same(tok_all.at[z, second], tok_all.at[z, first], tok_s.at[1], tok_r.at[1])
 
     def forward_tokens():
-        first, second = pl.ds(0, half_t), pl.ds(half_t, half_t)
-        return (
-            remote(tok_all.at[prv, first], tok_all.at[prv, first], tfw_s.at[0], tfw_r.at[0], nxt_dev),
-            remote(tok_all.at[nxt, second], tok_all.at[nxt, second], tfw_s.at[1], tfw_r.at[1], prv_dev),
-        )
-
-    def gather(c):
-        return (
-            remote(x_a.at[c, z], x_a.at[c, z], ag_s.at[c, 0], ag_r.at[c, 0], nxt_dev),
-            remote(x_a.at[c, z], x_a.at[c, z], ag_s.at[c, 1], ag_r.at[c, 1], prv_dev),
-        )
+        return same(tok_all.at[prv, first], tok_all.at[nxt, second], tfw_s, tfw_r)
+
+    def lead(c):
+        return same(x_a.at[c, z, low], x_a.at[c, z, high], ag_s.at[c, 0], ag_r.at[c, 0])
+
+    def rest(c):
+        return same(x_a.at[c, z, high], x_a.at[c, z, low], ag_s.at[c, 1], ag_r.at[c, 1])
 
     def forward(c):
-        return (
-            remote(x_a.at[c, prv, low], x_a.at[c, prv, low], fw_s.at[c, 0], fw_r.at[c, 0], nxt_dev),
-            remote(x_a.at[c, nxt, high], x_a.at[c, nxt, high], fw_s.at[c, 1], fw_r.at[c, 1], prv_dev),
-        )
-
-    def scatter_half(c):
-        return (
-            remote(part.at[c, far, low], half_in.at[c, 0], rh_s.at[c, 0], rh_r.at[c, 0], nxt_dev),
-            remote(part.at[c, far, high], half_in.at[c, 1], rh_s.at[c, 1], rh_r.at[c, 1], prv_dev),
-        )
-
-    def scatter_full(c):
-        return (
-            remote(part.at[c, nxt], full_in.at[c, 0], rf_s.at[c, 0], rf_r.at[c, 0], nxt_dev),
-            remote(part.at[c, prv], full_in.at[c, 1], rf_s.at[c, 1], rf_r.at[c, 1], prv_dev),
-        )
-
-    def mix_halves():
-        first, second = pl.ds(0, half_t), pl.ds(half_t, half_t)
-        return (
-            remote(mix.at[far, first], mix_half.at[0], mh_s.at[0], mh_r.at[0], nxt_dev),
-            remote(mix.at[far, second], mix_half.at[1], mh_s.at[1], mh_r.at[1], prv_dev),
-        )
-
-    def mix_fulls():
-        return (
-            remote(mix.at[nxt], mix_full.at[0], mf_s.at[0], mf_r.at[0], nxt_dev),
-            remote(mix.at[prv], mix_full.at[1], mf_s.at[1], mf_r.at[1], prv_dev),
-        )
+        return same(x_a.at[c, prv, low], x_a.at[c, nxt, high], fw_s.at[c], fw_r.at[c])
+
+    def scatter_far(c):
+        return both_ways(
+            part.at[c, far, low], half_in.at[c, 0], part.at[c, far, high], half_in.at[c, 1], rh_s.at[c], rh_r.at[c]
+        )
+
+    def scatter_pure(c):
+        return both_ways(
+            part.at[c, nxt, high], full_in.at[c, 0, high], part.at[c, prv, low], full_in.at[c, 1, low],
+            rf_s.at[c, 0], rf_r.at[c, 0],
+        )
+
+    def scatter_sum(c):
+        return both_ways(
+            part.at[c, nxt, low], full_in.at[c, 0, low], part.at[c, prv, high], full_in.at[c, 1, high],
+            rf_s.at[c, 1], rf_r.at[c, 1],
+        )
+
+    def mix_far():
+        return both_ways(mix.at[far, first], mix_half.at[0], mix.at[far, second], mix_half.at[1], mh_s, mh_r)
+
+    def mix_pure():
+        return both_ways(
+            mix.at[nxt, second], mix_full.at[0, second], mix.at[prv, first], mix_full.at[1, first],
+            mf_s.at[0], mf_r.at[0],
+        )
+
+    def mix_sum():
+        return both_ways(
+            mix.at[nxt, first], mix_full.at[0, first], mix.at[prv, second], mix_full.at[1, second],
+            mf_s.at[1], mf_r.at[1],
+        )
+
+    def start(*groups):
+        for group in groups:
+            for copy in group:
+                copy.start()
+
+    def await_in(*groups):
+        for group in groups:
+            for copy in group:
+                copy.wait_recv()
 
     def fill_a(c):
         @functools.partial(loop, plane)
@@ -180,14 +202,11 @@
                 pair = [wide32[pl.ds((s0 + d) * in_a + j, 8, stride=in_a), :] for d in (0, 8)]
                 x_a[c, z, pl.ds(s0, 16), cols] = jnp.concatenate(pair, axis=0).astype(bf16)
 
-        for copy in gather(c):
-            copy.start()
+        start(lead(c), rest(c))
 
     def stage_b(c):
-        for copy in gather(c):
-            copy.wait_recv()
-        for copy in forward(c):
-            copy.start()
+        await_in(lead(c))
+        start(forward(c))
 
     def stage_c(c):
         plane_b(c).wait_recv()
@@ -210,15 +229,14 @@
             acc[:, :hidden] += jnp.dot(rows_k, w_gate[span, :], preferred_element_type=f32)
             acc[:, hidden:] += jnp.dot(rows_k, w_up[span, :], preferred_element_type=f32)
 
-        @functools.partial(loop, LATE_IN)
+        @functools.partial(loop, LATE_IN, unroll=1)
         def _(k):
             here = pl.ds(pl.multiple_of(k * block, LANES), block)
             contract(x_b[:, here], pl.ds(pl.multiple_of((PARTS - LATE_IN + k) * block, LANES), block))
 
-        for copy in forward(c):
-            copy.wait_recv()
-
-        @functools.partial(loop, PARTS - LATE_IN)
+        await_in(rest(c), forward(c))
+
+        @functools.partial(loop, PARTS - LATE_IN, unroll=1)
         def _(k):
             here = pl.ds(pl.multiple_of(k * block, LANES), block)
             contract(x_a[c, :, :, here].reshape(rows, block), here)
@@ -226,16 +244,7 @@
         gate = acc[:, :hidden]
         hid[...] = (gate / (1.0 + jnp.exp(-gate)) * acc[:, hidden:]).astype(bf16)
 
-        @functools.partial(loop, PARTS - LATE_OUT)
-        def _(k):
-            span = pl.ds(pl.multiple_of(k * block, LANES), block)
-            value = jnp.dot(hid[...], w_down[:, span], preferred_element_type=f32)
-            part[c, :, :, span] = value.astype(bf16).reshape(SHARDS, plane, block)
-
-        for copy in scatter_half(c):
-            copy.start()
-
-        @functools.partial(loop, LATE_OUT)
+        @functools.partial(loop, LATE_OUT, unroll=1)
         def _(k):
             span = pl.ds(pl.multiple_of((PARTS - LATE_OUT + k) * block, LANES), block)
             value = jnp.dot(hid[...], w_down[:, span], preferred_element_type=f32)
@@ -253,18 +262,23 @@
 
         spread(back_b, home_b, bb_s, bb_r, c)
 
+        @functools.partial(loop, PARTS - LATE_OUT, unroll=1)
+        def _(k):
+            span = pl.ds(pl.multiple_of(k * block, LANES), block)
+            value = jnp.dot(hid[...], w_down[:, span], preferred_element_type=f32)
+            part[c, :, :, span] = value.astype(bf16).reshape(SHARDS, plane, block)
+
+        start(scatter_far(c), scatter_pure(c))
+
     def stage_e(c):
-        for copy in scatter_half(c):
-            copy.wait_recv()
+        await_in(scatter_far(c))
         for side, owner, span in ((0, nxt, low), (1, prv, high)):
             mine = part[c, owner, span].astype(f32)
             part[c, owner, span] = (mine + half_in[c, side].astype(f32)).astype(bf16)
-        for copy in scatter_full(c):
-            copy.start()
+        start(scatter_sum(c))
 
     def stage_f(c):
-        for copy in scatter_full(c):
-            copy.wait_recv()
+        await_in(scatter_pure(c), scatter_sum(c))
 
         @functools.partial(loop, out_a)
         def _(j):
@@ -322,34 +336,37 @@
             itab_in[2 + k:3 + k, 0:count] = where
             ftab_in[k:k + 1, 0:count] = weights[k:k + 1, :]
 
-    own_tables()
-
-    @functools.partial(loop, subs)
-    def _(j):
+    def unpack(j):
         cols = pl.ds(pl.multiple_of(j * LANES, LANES), LANES)
         for t0 in range(0, count, 16):
             value = tok_ref[pl.ds(t0, 16), cols].astype(f32)
             for d in (0, 8):
                 wide32[pl.ds((t0 + d) * subs + j, 8, stride=subs), :] = value[d:d + 8]
 
+    loop(subs, unpack, start=in_a)
+
+    @functools.partial(loop, count)
+    def _(t):
+        tok_all[z, t] = wide32[pl.ds(pl.multiple_of(t * subs + in_a, 8), in_b), :].astype(bf16)
+
+    own_tables()
+    pl.semaphore_wait(barrier, plane + 2)
+    start(lead_tokens(), rest_tokens())
     own_moves = [
         pltpu.make_async_copy(itab_in, itab.at[z], tab_l.at[0]),
         pltpu.make_async_copy(ftab_in, ftab.at[z], tab_l.at[1]),
     ]
     for move in own_moves:
         move.start()
+    loop(in_a, unpack)
 
     @functools.partial(loop, count)
     def _(t):
-        tok_all[z, t] = wide32[pl.ds(pl.multiple_of(t * subs + in_a, 8), in_b), :].astype(bf16)
         tok_a[t] = wide32[pl.ds(pl.multiple_of(t * subs, 8), in_a), :].astype(bf16)
 
     for move in own_moves:
         move.wait()
     fill_a(0)
-    pl.semaphore_wait(barrier, plane + 2)
-    for copy in gather_tokens():
-        copy.start()
     for copy in tables():
         copy.start()
     launch_a(0)
@@ -357,10 +374,8 @@
         fill_a(c)
         if c < 3:
             launch_a(c)
-    for copy in gather_tokens():
-        copy.wait_recv()
-    for copy in forward_tokens():
-        copy.start()
+    await_in(lead_tokens())
+    start(forward_tokens())
 
     def ready():
         for copy in tables():
@@ -373,8 +388,7 @@
             move.start()
         for move in moves:
             move.wait()
-        for copy in forward_tokens():
-            copy.wait_recv()
+        await_in(rest_tokens(), forward_tokens())
         for copy in w_copies:
             copy.wait()
 
@@ -399,30 +413,30 @@
             def _(stage=stage, c=c):
                 stage(c)
 
-    loop(MOST + 3, run)
-
-    @functools.partial(loop, MOST)
+    loop(MOST + 2, run, unroll=1)
+    stage_e(MOST - 1)
+
+    @functools.partial(loop, MOST, unroll=1)
     def _(c):
         return_b(c).wait_recv()
 
     mix_one(far)
-    for copy in mix_halves():
-        copy.start()
+    start(mix_far())
     mix_one(nxt)
     mix_one(prv)
+    start(mix_pure())
+    stage_f(MOST - 2)
     mix_one(z)
-    stage_f(MOST - 1)
-    for copy in mix_halves():
-        copy.wait_recv()
-    for side, owner, start in ((0, nxt, 0), (1, prv, half_t)):
+    await_in(mix_far())
+    for side, owner, begin in ((0, nxt, 0), (1, prv, half_t)):
         @functools.partial(loop, half_t)
         def _(t):
-            mix[owner, start + t] = (mix[owner, start + t].astype(f32) + mix_half[side, t].astype(f32)).astype(bf16)
-
-    for copy in mix_fulls():
-        copy.start()
-
-    @functools.partial(loop, MOST)
+            mix[owner, begin + t] = (mix[owner, begin + t].astype(f32) + mix_half[side, t].astype(f32)).astype(bf16)
+
+    start(mix_sum())
+    stage_f(MOST - 1)
+
+    @functools.partial(loop, MOST, unroll=1)
     def _(c):
         return_a(c).wait_recv()
 
@@ -438,8 +452,7 @@
             out_ref[pl.ds(t0, 16), cols] = jnp.concatenate(pair, axis=0).astype(bf16)
 
     loop(out_a, settle)
-    for copy in mix_fulls():
-        copy.wait_recv()
+    await_in(mix_pure(), mix_sum())
 
     @functools.partial(loop, count)
     def _(t):
@@ -447,14 +460,16 @@
         wide32[pl.ds(pl.multiple_of(t * subs + out_a, 8), out_b), :] = total
 
     loop(subs, settle, start=out_a)
-    for copy in (*tables(), *gather_tokens(), *forward_tokens(), *mix_halves(), *mix_fulls()):
+    for copy in (
+        *tables(), *lead_tokens(), *rest_tokens(), *forward_tokens(), *mix_far(), *mix_pure(), *mix_sum()
+    ):
         copy.wait_send()
 
-    @functools.partial(loop, MOST)
+    @functools.partial(loop, MOST, unroll=1)
     def _(c):
         for copy in (plane_a(c), plane_b(c), return_a(c), return_b(c)):
             copy.wait_send()
-        for group in (gather, forward, scatter_half, scatter_full):
+        for group in (lead, rest, forward, scatter_far, scatter_pure, scatter_sum):
             for copy in group(c):
                 copy.wait_send()
 
@@ -507,18 +522,18 @@
             vmem((SHARDS * plane, hidden), bf16),
             dma((3,)),
             dma((3, 2)), dma((3, 2)), dma((8,)),
-            dma((2,)), dma((2,)),
+            dma((2, 2)), dma((2, 2)),
             dma((2,)), dma((2,)),
             dma((MOST,)), dma((MOST,)),
             dma((MOST,)), dma((MOST,)),
+            dma((MOST, 2, 2)), dma((MOST, 2, 2)),
             dma((MOST, 2)), dma((MOST, 2)),
             dma((MOST, 2)), dma((MOST, 2)),
-            dma((MOST, 2)), dma((MOST, 2)),
-            dma((MOST, 2)), dma((MOST, 2)),
+            dma((MOST, 2, 2)), dma((MOST, 2, 2)),
             dma((MOST,)), dma((MOST,)),
             dma((MOST,)), dma((MOST,)),
             dma((2,)), dma((2,)),
-            dma((2,)), dma((2,)),
+            dma((2, 2)), dma((2, 2)),
         ],
         compiler_params=pltpu.CompilerParams(
             collective_id=0, has_side_effects=True, vmem_limit_bytes=67043328

time: 139 us -> 135 us (0.971); the launches traced: 137 us -> 135 us
  Pallas kernels: 135 us -> 133 us
    pallas_call x1, Pallas kernels: 135 us -> 133 us  [per_device(): pl.pallas_call(functools.partial(kernel, plane, count, block), out_shape=...]
where the time goes in v4:
time: 135 us
  Pallas kernels  133 us (99%)
  local copies, waits for them, and re-layouts  2.16 us (2%)
    pallas_call x1, Pallas kernels, per_device(): pl.pallas_call(functools.partial(kernel, plane, count, block), out_shape=...  133 us

profile of v4, /device:TPU:1, one launch (start us, length us, event | category | flops | bytes accessed | tf_op | source)
XLA Modules:
  0.0 134.9 jit_solution(6705212097613637807)
XLA Ops:
  0.0 132.7 %shard_map.64 = bf16[64,7168]{1,0:T(8,128)(2,1)} custom-call(s32[2,64]{1,0:T(2,128)} %bitcast.2, f32[2,64]{1,0:T(2,128)} %bitcast.3, bf16[64,7168]{1,0:T(8,128)(2,1)} %tok_ref.1, bf16[1,7168,512]{2,1,0:T(8,128)(2,1)} %gate_hbm.1, bf16[1,7168,512]{2,1,0:T(8,128)(2,1)} %up_hbm.1, bf16[1,512,7168]{2,1,0:T(8,128)(2,1)} %down_hbm.1), custom_call_target="tpu_custom_call" | custom-call | tf_op jit(solution)/shard_map/pallas_call | solution.py:487
  132.7 2.2 %copy.8 = bf16[64,7168]{1,0:T(8,128)(2,1)} copy(bf16[64,7168]{1,0:T(8,128)(2,1)} %shard_map.64) | data formatting | bytes 1835008

commit v5 on v4

--- a/solution.py
+++ b/solution.py
@@ -59,15 +59,23 @@
     for copy in w_copies:
         copy.start()
 
-    def peer(k):
-        other = lax.rem(me + k, plane)
-        return other, (other // ys, (other % ys) * SHARDS + z)
+    chips = plane // (2 * ys)
+    x, core = node // 2, node % 2
+
+    def hops(step):
+        return min(step[0], chips - step[0]) + min(step[2], ys - step[2])
+
+    steps = [(dx, dc, dy) for dx in range(chips) for dc in range(2) for dy in range(ys)][1:]
+    steps.sort(key=hops, reverse=True)
+    peers = []
+    for dx, dc, dy in steps:
+        other_node, other_y = ((x + dx) % chips) * 2 + (core + dc) % 2, (y + dy) % ys
+        peers.append((other_node * ys + other_y, (other_node, other_y * SHARDS + z)))
 
     barrier = pltpu.get_barrier_semaphore()
 
-    @functools.partial(loop, plane, start=1, unroll=plane - 1)
-    def _(k):
-        pl.semaphore_signal(barrier, inc=1, device_id=peer(k)[1], device_id_type=MESH)
+    for _, dev in peers:
+        pl.semaphore_signal(barrier, inc=1, device_id=dev, device_id_type=MESH)
 
     for dev in z_devs:
         pl.semaphore_signal(barrier, inc=1, device_id=dev, device_id_type=MESH)
@@ -78,11 +86,8 @@
         )
 
     def spread(src, dst, s_sem, r_sem, c):
-        @functools.partial(loop, plane, start=1, unroll=plane - 1)
-        def _(k):
-            other, dev = peer(k)
+        for other, dev in peers:
             remote(src.at[c, other], dst.at[c, me], s_sem.at[c], r_sem.at[c], dev).start()
-
         dst[c, me] = src[c, me]
 
     def spread_all(src, dst, s_sem, r_sem, c):
@@ -422,10 +427,11 @@
 
     mix_one(far)
     start(mix_far())
+    stage_f(MOST - 2)
     mix_one(nxt)
     mix_one(prv)
     start(mix_pure())
-    stage_f(MOST - 2)
+    stage_f(MOST - 1)
     mix_one(z)
     await_in(mix_far())
     for side, owner, begin in ((0, nxt, 0), (1, prv, half_t)):
@@ -434,7 +440,6 @@
             mix[owner, begin + t] = (mix[owner, begin + t].astype(f32) + mix_half[side, t].astype(f32)).astype(bf16)
 
     start(mix_sum())
-    stage_f(MOST - 1)
 
     @functools.partial(loop, MOST, unroll=1)
     def _(c):

time: 135 us -> 135 us (level)
  no operation moved by 1% of the time
where the time goes in v5:
time: 135 us; the launch traced here: 134 us
  Pallas kernels  132 us (98%)
  local copies, waits for them, and re-layouts  2.16 us (2%)
    pallas_call x1, Pallas kernels, per_device(): pl.pallas_call(functools.partial(kernel, plane, count, block), out_shape=...  132 us

profile of v5, /device:TPU:1, one launch (start us, length us, event | category | flops | bytes accessed | tf_op | source)
XLA Modules:
  0.0 134.4 jit_solution(5527383411855204301)
XLA Ops:
  0.0 132.2 %shard_map.64 = bf16[64,7168]{1,0:T(8,128)(2,1)} custom-call(s32[2,64]{1,0:T(2,128)} %bitcast.2, f32[2,64]{1,0:T(2,128)} %bitcast.3, bf16[64,7168]{1,0:T(8,128)(2,1)} %tok_ref.1, bf16[1,7168,512]{2,1,0:T(8,128)(2,1)} %gate_hbm.1, bf16[1,7168,512]{2,1,0:T(8,128)(2,1)} %up_hbm.1, bf16[1,512,7168]{2,1,0:T(8,128)(2,1)} %down_hbm.1), custom_call_target="tpu_custom_call" | custom-call | tf_op jit(solution)/shard_map/pallas_call | solution.py:492
  132.2 2.2 %copy.8 = bf16[64,7168]{1,0:T(8,128)(2,1)} copy(bf16[64,7168]{1,0:T(8,128)(2,1)} %shard_map.64) | data formatting | bytes 1835008
